TPU v7x, 32 devices: a whole 2x2x4 slice. The times are simulated.
32 devices in a mesh: batch: 2 (over x), rows: 16 (over z, y, core).
Axes of the slice: x: 2, y: 2, z: 4, core: 2. Of those that a mesh axis runs over, the one named last changes fastest.
Arguments:
- latent: bfloat16 [16, 192, 256], P(None, ('batch', 'rows')), parts along dimension 1, may hold values from -11 to 11
- kernel_in: bfloat16 [3, 3, 16, 512], replicated, may hold values from -0.5 to 0.5
- gain_one: float32 [512], replicated, may hold values from 0.25 to 1.75
- bias_one: float32 [512], replicated, may hold values from -3 to 3
- kernel_one: bfloat16 [3, 3, 512, 512], replicated, may hold values from -0.09375 to 0.09375
- gain_two: float32 [512], replicated, may hold values from 0.25 to 1.75
- bias_two: float32 [512], replicated, may hold values from -3 to 3
- kernel_two: bfloat16 [3, 3, 512, 512], replicated, may hold values from -0.09375 to 0.09375
Outputs:
- block_out: bfloat16 [192, 256, 512], P(('batch', 'rows')), parts along dimension 0
There are 2 independent parts, one for each index of `batch`. A program takes and returns all parts, laid end to end along the dimension named above; an argument that names none is the same for every part. Nothing has to cross between parts.
All inputs are finite; a program needn't handle non-finite values.
Results may differ from a plain program's by a relative error of at most 0.014.
Values may be sent and summed in bfloat16 or wider, within the bound.
A program may use at most 64 MiB of HBM per device.

v0:
```python
import jax
import jax.numpy as jnp
from jax import lax
from jax.sharding import PartitionSpec as P

GROUPS = 32


EPSILON = 1e-06


def extended(cells, sides, width):
    for axis, dim in sides:
        count = lax.axis_size(axis)
        ends = count - 1
        head = lax.slice_in_dim(cells, 0, width, axis=dim)
        tail = lax.slice_in_dim(cells, cells.shape[dim] - width, cells.shape[dim], axis=dim)
        cells = jnp.concatenate(
            [
                lax.ppermute(tail, axis, [(i, (i + 1) % count) for i in range(ends)]),
                cells,
                lax.ppermute(head, axis, [((i + 1) % count, i) for i in range(ends)]),
            ],
            axis=dim,
        )
    return cells


def convolve(padded, kernel):
    height = padded.shape[0] - 2
    width = padded.shape[1] - 2
    inputs = padded.shape[2]
    total = jnp.zeros((height * width, kernel.shape[3]), jnp.float32)
    for row_shift in range(3):
        band = padded[row_shift : row_shift + height]
        stacked = jnp.concatenate(
            [band[:, col_shift : col_shift + width] for col_shift in range(3)], axis=-1
        )
        total = total + jnp.dot(
            stacked.reshape(height * width, 3 * inputs),
            kernel[row_shift].reshape(3 * inputs, -1),
            preferred_element_type=jnp.float32,
        )
    return total.reshape(height, width, -1)


def pad_columns(field):
    return jnp.pad(field, ((0, 0), (1, 1), (0, 0)))


def moments(own):
    values = own.astype(jnp.float32).reshape(own.shape[0], own.shape[1], GROUPS, -1)
    count = values.shape[0] * values.shape[1] * values.shape[3] * lax.axis_size("rows")
    totals, squares = lax.psum(
        (jnp.sum(values, axis=(0, 1, 3)), jnp.sum(values * values, axis=(0, 1, 3))), "rows"
    )
    center = totals / count
    spread = squares / count - center * center
    return (center, spread)


def activate(field, center, spread, gain, bias):
    values = field.astype(jnp.float32).reshape(field.shape[0], field.shape[1], GROUPS, -1)
    normed = (values - center[None, None, :, None]) * lax.rsqrt(spread + EPSILON)[
        None, None, :, None
    ]
    normed = normed.reshape(field.shape) * gain + bias
    return jax.nn.silu(normed).astype(jnp.bfloat16)


def act_halo(field):
    return extended(field, (("rows", 0),), 1)


def local(latent, kernel_in, gain_one, bias_one, kernel_one, gain_two, bias_two, kernel_two):
    padded = extended(latent, (("rows", 1),), 1)
    features = convolve(pad_columns(jnp.transpose(padded, (1, 2, 0))), kernel_in).astype(
        jnp.bfloat16
    )
    center, spread = moments(features)
    first = activate(features, center, spread, gain_one, bias_one)
    hidden = convolve(pad_columns(act_halo(first)), kernel_one).astype(jnp.bfloat16)
    center, spread = moments(hidden)
    second = activate(hidden, center, spread, gain_two, bias_two)
    result = features.astype(jnp.float32) + convolve(pad_columns(act_halo(second)), kernel_two)
    return result.astype(jnp.bfloat16)


def solution(mesh):
    in_specs = (P(None, ("batch", "rows"), None), P(), P(), P(), P(), P(), P(), P())
    out_specs = P(("batch", "rows"), None, None)
    return jax.shard_map(local, mesh=mesh, in_specs=in_specs, out_specs=out_specs, check_vma=False)
```

profile of v0, /device:TPU:0, one launch (start us, length us, event | category | flops | bytes accessed | tf_op | source)
XLA Modules:
  0.0 123.9 jit_solution(13918221155748447590)
XLA Ops:
  0.0 0.7 fusion.29
  0.7 2.4 %collective-permute-start = (bf16[16,1,256]{2,0,1:T(8,128)(2,1)S(1)}, bf16[16,1,256]{2,0,1:T(8,128)(2,1)S(1)}, u32[]{:S(2)}, u32[]{:S(2)}) collective-permute-start(bf16[16,1,256]{2,0,1:T(8,128)(2,1)S(1)} %get-tuple-element.53), channel_id=1, source_target_pairs={{0,1},{1,2},{2,3},{3,4},{4,5},{5,6},{6,7},{7,8},{8,9},{9,10},{10,1... | collective-permute-start | bytes 24584 | tf_op jit(solution)/shard_map/ppermute | solution.py:20
  3.1 1.3 %collective-permute-start.1 = (bf16[16,1,256]{2,0,1:T(8,128)(2,1)S(1)}, bf16[16,1,256]{2,0,1:T(8,128)(2,1)S(1)}, u32[]{:S(2)}, u32[]{:S(2)}) collective-permute-start(bf16[16,1,256]{2,0,1:T(8,128)(2,1)S(1)} %get-tuple-element.54), channel_id=1, source_target_pairs={{1,0},{2,1},{3,2},{4,3},{5,4},{6,5},{7,6},{8,7},{9,8},{10,9},{11,1... | collective-permute-start | bytes 24584 | tf_op jit(solution)/shard_map/ppermute | solution.py:22
  4.4 0.9 fusion.28
  5.3 0.0 collective-permute-done
  5.3 3.0 %collective-permute-done.1 = bf16[16,1,256]{2,0,1:T(8,128)(2,1)S(1)} collective-permute-done((bf16[16,1,256]{2,0,1:T(8,128)(2,1)S(1)}, bf16[16,1,256]{2,0,1:T(8,128)(2,1)S(1)}, u32[]{:S(2)}, u32[]{:S(2)}) %collective-permute-start.1) | collective-permute-done | bytes 8224 | tf_op jit(solution)/shard_map/ppermute | solution.py:22
  8.3 0.8 maximum_bitcast_fusion.3
  9.1 0.1 pad_slice_fusion.1
  9.4 0.6 fusion.30
  10.0 0.6 convolution_add_fusion.1
  10.6 0.0 copy-start
  10.6 0.0 copy-start.1
  10.6 0.6 fusion.21
  11.2 0.1 reduce_sum.47
  11.3 0.1 reduce_sum.53
  11.4 0.1 reduce_sum.51
  11.5 0.1 reduce_sum.54
  11.6 32.8 %all-reduce.4 = (f32[32]{0:T(128)S(1)}, f32[32]{0:T(128)S(1)}) all-reduce(f32[32]{0:T(128)S(1)} %reduce_sum.54, f32[32]{0:T(128)S(1)} %reduce_sum.51), channel_id=1, replica_groups=mesh['batch'=2,'rows'=16] {'rows'}, use_global_device_ids=true, to_apply=%region_5.6 | all-reduce | flops 64 | bytes 512 | tf_op jit(solution)/shard_map/psum | solution.py:54
  44.4 0.1 mul.65
  44.5 0.1 mul.66
  44.5 0.1 sub.32
  44.6 0.1 sub.33
  44.7 0.0 copy-done
  44.7 0.0 copy-done.1
  44.7 1.0 multiply_convert_fusion.1
  45.7 1.3 %collective-permute-start.2 = (bf16[1,256,512]{2,1,0:T(8,128)(2,1)S(1)}, bf16[1,256,512]{2,1,0:T(8,128)(2,1)S(1)}, u32[]{:S(2)}, u32[]{:S(2)}) collective-permute-start(bf16[1,256,512]{2,1,0:T(8,128)(2,1)S(1)} %get-tuple-element.39), channel_id=1, source_target_pairs={{0,1},{1,2},{2,3},{3,4},{4,5},{5,6},{6,7},{7,8},{8,9},{9,10},{10,1... | collective-permute-start | bytes 786440 | tf_op jit(solution)/shard_map/ppermute | solution.py:20
  47.1 1.3 %collective-permute-start.3 = (bf16[1,256,512]{2,1,0:T(8,128)(2,1)S(1)}, bf16[1,256,512]{2,1,0:T(8,128)(2,1)S(1)}, u32[]{:S(2)}, u32[]{:S(2)}) collective-permute-start(bf16[1,256,512]{2,1,0:T(8,128)(2,1)S(1)} %get-tuple-element.40), channel_id=1, source_target_pairs={{1,0},{2,1},{3,2},{4,3},{5,4},{6,5},{7,6},{8,7},{9,8},{10,9},{11,1... | collective-permute-start | bytes 786440 | tf_op jit(solution)/shard_map/ppermute | solution.py:22
  48.4 4.0 %fusion.23 = (bf16[1,3,512,512]{3,2,1,0:T(8,128)(2,1)S(1)}, bf16[1,3,512,512]{3,2,1,0:T(8,128)(2,1)S(1)}, bf16[1,3,512,512]{3,2,1,0:T(8,128)(2,1)}) fusion(bf16[3,3,512,512]{3,2,1,0:T(8,128)(2,1)} %param.12), kind=kLoop, calls=%fused_computation.56 | loop fusion | bytes 9437184 | tf_op jit(solution)/shard_map/slice | solution.py:41
  52.3 0.0 collective-permute-done.2
  52.3 0.0 collective-permute-done.3
  52.3 0.5 fusion.19
  52.9 1.8 %fusion.25 = (bf16[6,256,512]{2,1,0:T(8,128)(2,1)S(1)}, bf16[6,256,512]{2,1,0:T(8,128)(2,1)S(1)}, bf16[6,256,512]{2,1,0:T(8,128)(2,1)S(1)}, bf16[6,256,512]{2,1,...) fusion(bf16[8,258,512]{2,1,0:T(8,128)(2,1)S(1)} %fusion.19), kind=kLoop, calls=%fused_computation.58 | loop fusion | bytes 18874368 | tf_op jit(solution)/shard_map/slice | solution.py:37
  54.7 1.7 %fusion.7 = (bf16[6,256,1536]{2,1,0:T(8,128)(2,1)S(1)}, bf16[6,256,1536]{2,1,0:T(8,128)(2,1)S(1)}, bf16[6,256,1536]{2,1,0:T(8,128)(2,1)S(1)}) fusion(bf16[6,256,512]{2,1,0:T(8,128)(2,1)S(1)} %multiply_convert_fusion.1, bf16[1,256,512]{2,1,0:T(8,128)(2,1)S(1)} %collective-permute-done.2, bf16[6,256,512]{2,1,0:T(8,128)(2,1)S(1)} %get-tuple-element.29, ...), kind=kLoop, calls=%fused_computation.13 | loop fusion | flops 51904512 | bytes 25690112 | tf_op jit(solution)/shard_map/concatenate | solution.py:36
  56.4 4.0 %fusion.31 = f32[1536,512]{1,0:T(8,128)S(1)} fusion(bf16[1536,1536]{1,0:T(8,128)(2,1)S(1)} %bitcast.53, bf16[1536,512]{1,0:T(8,128)(2,1)} %bitcast.61), kind=kOutput, calls=%fused_computation.64 | convolution fusion | flops 2415919104 | bytes 9437184 | tf_op jit(solution)/shard_map/dot_general | solution.py:39
  60.4 2.6 %fusion.32 = f32[1536,512]{1,0:T(8,128)S(1)} fusion(bf16[1536,1536]{1,0:T(8,128)(2,1)S(1)} %bitcast.51, bf16[1536,512]{1,0:T(8,128)(2,1)S(1)} %bitcast.59), kind=kOutput, calls=%fused_computation.65 | convolution fusion | flops 2415919104 | bytes 9437184 | tf_op jit(solution)/shard_map/dot_general | solution.py:39
  63.0 0.0 copy-start.2
  63.0 0.0 copy-start.3
  63.0 4.6 %fusion.20 = (f32[512]{0:T(512)S(1)}, f32[512]{0:T(512)S(1)}, f32[1536,512]{1,0:T(8,128)}) fusion(f32[1536,512]{1,0:T(8,128)S(1)} %fusion.32, f32[1536,512]{1,0:T(8,128)S(1)} %fusion.31, bf16[1536,1536]{1,0:T(8,128)(2,1)S(1)} %bitcast.49, bf16[1536,512]{1,0:T(8,128)(2,1)S(1)} %bitcast.57), kind=kOutput, calls=%fused_computation.53 | convolution fusion | flops 2421423104 | bytes 15732736 | tf_op jit(solution)/shard_map/dot_general | solution.py:39
  67.6 0.1 reduce_sum.59
  67.7 0.1 reduce_sum.72
  67.8 0.1 reduce_sum.74
  67.9 0.1 reduce_sum.75
  68.0 30.7 %all-reduce.3 = (f32[32]{0:T(128)S(1)}, f32[32]{0:T(128)S(1)}) all-reduce(f32[32]{0:T(128)S(1)} %reduce_sum.75, f32[32]{0:T(128)S(1)} %reduce_sum.72), channel_id=1, replica_groups=mesh['batch'=2,'rows'=16] {'rows'}, use_global_device_ids=true, to_apply=%region_11.12 | all-reduce | flops 64 | bytes 512 | tf_op jit(solution)/shard_map/psum | solution.py:54
  98.7 0.1 mul.74
  98.8 0.1 mul.75
  98.9 0.1 sub.37
  98.9 0.1 sub.38
  99.0 0.0 copy-done.2
  99.0 0.0 copy-done.3
  99.0 2.9 %multiply_convert_fusion = bf16[6,256,512]{2,1,0:T(8,128)(2,1)S(1)} fusion(f32[6,256,512]{2,1,0:T(8,128)} %bitcast.55, f32[512]{0:T(512)S(1)} %copy-done.2, f32[512]{0:T(512)S(1)} %copy-done.3, f32[512]{0:T(512)S(1)} %mul.75, f32[512]{0:T(512)S(1)} %sub.38), kind=kLoop, calls=%fused_computation.24 | loop fusion | flops 7077888 | bytes 4726784 | tf_op jit(solution)/shard_map/convert_element_type | solution.py:68
  102.0 1.5 %collective-permute-start.4 = (bf16[1,256,512]{2,1,0:T(8,128)(2,1)S(1)}, bf16[1,256,512]{2,1,0:T(8,128)(2,1)S(1)}, u32[]{:S(2)}, u32[]{:S(2)}) collective-permute-start(bf16[1,256,512]{2,1,0:T(8,128)(2,1)S(1)} %get-tuple-element.34), channel_id=1, source_target_pairs={{0,1},{1,2},{2,3},{3,4},{4,5},{5,6},{6,7},{7,8},{8,9},{9,10},{10,1... | collective-permute-start | bytes 786440 | tf_op jit(solution)/shard_map/ppermute | solution.py:20
  103.4 1.3 %collective-permute-start.5 = (bf16[1,256,512]{2,1,0:T(8,128)(2,1)S(1)}, bf16[1,256,512]{2,1,0:T(8,128)(2,1)S(1)}, u32[]{:S(2)}, u32[]{:S(2)}) collective-permute-start(bf16[1,256,512]{2,1,0:T(8,128)(2,1)S(1)} %get-tuple-element.35), channel_id=1, source_target_pairs={{1,0},{2,1},{3,2},{4,3},{5,4},{6,5},{7,6},{8,7},{9,8},{10,9},{11,1... | collective-permute-start | bytes 786440 | tf_op jit(solution)/shard_map/ppermute | solution.py:22
  104.7 4.0 %fusion.22 = (bf16[1,3,512,512]{3,2,1,0:T(8,128)(2,1)S(1)}, bf16[1,3,512,512]{3,2,1,0:T(8,128)(2,1)S(1)}, bf16[1,3,512,512]{3,2,1,0:T(8,128)(2,1)}) fusion(bf16[3,3,512,512]{3,2,1,0:T(8,128)(2,1)} %param.15), kind=kLoop, calls=%fused_computation.55 | loop fusion | bytes 9437184 | tf_op jit(solution)/shard_map/slice | solution.py:41
  108.7 0.0 collective-permute-done.4
  108.7 0.0 collective-permute-done.5
  108.7 0.5 select_maximum_fusion
  109.3 1.8 %fusion.24 = (bf16[6,256,512]{2,1,0:T(8,128)(2,1)S(1)}, bf16[6,256,512]{2,1,0:T(8,128)(2,1)S(1)}, bf16[6,256,512]{2,1,0:T(8,128)(2,1)S(1)}, bf16[6,256,512]{2,1,...) fusion(bf16[8,258,512]{2,1,0:T(8,128)(2,1)S(1)} %select_maximum_fusion), kind=kLoop, calls=%fused_computation.57 | loop fusion | bytes 18874368 | tf_op jit(solution)/shard_map/slice | solution.py:37
  111.0 1.7 %fusion.3 = (bf16[6,256,1536]{2,1,0:T(8,128)(2,1)S(1)}, bf16[6,256,1536]{2,1,0:T(8,128)(2,1)S(1)}, bf16[6,256,1536]{2,1,0:T(8,128)(2,1)S(1)}) fusion(bf16[6,256,512]{2,1,0:T(8,128)(2,1)S(1)} %multiply_convert_fusion, bf16[1,256,512]{2,1,0:T(8,128)(2,1)S(1)} %collective-permute-done.4, bf16[6,256,512]{2,1,0:T(8,128)(2,1)S(1)} %get-tuple-element.23, ...), kind=kLoop, calls=%fused_computation.7 | loop fusion | flops 51904512 | bytes 25690112 | tf_op jit(solution)/shard_map/concatenate | solution.py:36
  112.7 4.0 %fusion.33 = f32[1536,512]{1,0:T(8,128)S(1)} fusion(bf16[1536,1536]{1,0:T(8,128)(2,1)S(1)} %bitcast.54, bf16[1536,512]{1,0:T(8,128)(2,1)} %bitcast.62), kind=kOutput, calls=%fused_computation.66 | convolution fusion | flops 2415919104 | bytes 9437184 | tf_op jit(solution)/shard_map/dot_general | solution.py:39
  116.8 2.6 %fusion.34 = f32[1536,512]{1,0:T(8,128)S(1)} fusion(bf16[1536,1536]{1,0:T(8,128)(2,1)S(1)} %bitcast.52, bf16[1536,512]{1,0:T(8,128)(2,1)S(1)} %bitcast.60), kind=kOutput, calls=%fused_computation.67 | convolution fusion | flops 2415919104 | bytes 9437184 | tf_op jit(solution)/shard_map/dot_general | solution.py:39
  119.4 2.8 %fusion.9 = f32[1536,512]{1,0:T(8,128)S(1)} fusion(f32[1536,512]{1,0:T(8,128)S(1)} %fusion.34, f32[1536,512]{1,0:T(8,128)S(1)} %fusion.33, bf16[1536,1536]{1,0:T(8,128)(2,1)S(1)} %bitcast.50, bf16[1536,512]{1,0:T(8,128)(2,1)S(1)} %bitcast.58), kind=kOutput, calls=%fused_computation.20 | convolution fusion | flops 2417491968 | bytes 15728640 | tf_op jit(solution)/shard_map/dot_general | solution.py:39
  122.2 1.7 %add_convert_fusion = bf16[6,256,512]{2,1,0:T(8,128)(2,1)} fusion(f32[6,256,512]{2,1,0:T(8,128)S(1)} %bitcast.48, f32[6,256,512]{2,1,0:T(8,128)S(1)} %bitcast.56), kind=kLoop, calls=%fused_computation.23 | loop fusion | flops 1572864 | bytes 7864320 | tf_op jit(solution)/shard_map/convert_element_type | solution.py:86
  (9 shorter events, 0.2 us)
Async XLA Ops:
  0.7 4.6 %collective-permute-start = (bf16[16,1,256]{2,0,1:T(8,128)(2,1)S(1)}, bf16[16,1,256]{2,0,1:T(8,128)(2,1)S(1)}, u32[]{:S(2)}, u32[]{:S(2)}) collective-permute-start(bf16[16,1,256]{2,0,1:T(8,128)(2,1)S(1)} %get-tuple-element.53), channel_id=1, source_target_pairs={{0,1},{1,2},{2,3},{3,4},{4,5},{5,6},{6,7},{7,8},{8,9},{9,10},{10,1... | collective-permute-start | bytes 24584 | tf_op jit(solution)/shard_map/ppermute | solution.py:20
  3.1 5.2 %collective-permute-start.1 = (bf16[16,1,256]{2,0,1:T(8,128)(2,1)S(1)}, bf16[16,1,256]{2,0,1:T(8,128)(2,1)S(1)}, u32[]{:S(2)}, u32[]{:S(2)}) collective-permute-start(bf16[16,1,256]{2,0,1:T(8,128)(2,1)S(1)} %get-tuple-element.54), channel_id=1, source_target_pairs={{1,0},{2,1},{3,2},{4,3},{5,4},{6,5},{7,6},{8,7},{9,8},{10,9},{11,1... | collective-permute-start | bytes 24584 | tf_op jit(solution)/shard_map/ppermute | solution.py:22
  10.6 34.1 %copy-start = (f32[512]{0:T(512)S(1)}, f32[512]{0:T(512)}, u32[]{:S(2)}) copy-start(f32[512]{0:T(512)} %param.11) | copy-start | bytes 6148
  10.6 34.1 %copy-start.1 = (f32[512]{0:T(512)S(1)}, f32[512]{0:T(512)}, u32[]{:S(2)}) copy-start(f32[512]{0:T(512)} %param.10) | copy-start | bytes 6148
  45.7 6.6 %collective-permute-start.2 = (bf16[1,256,512]{2,1,0:T(8,128)(2,1)S(1)}, bf16[1,256,512]{2,1,0:T(8,128)(2,1)S(1)}, u32[]{:S(2)}, u32[]{:S(2)}) collective-permute-start(bf16[1,256,512]{2,1,0:T(8,128)(2,1)S(1)} %get-tuple-element.39), channel_id=1, source_target_pairs={{0,1},{1,2},{2,3},{3,4},{4,5},{5,6},{6,7},{7,8},{8,9},{9,10},{10,1... | collective-permute-start | bytes 786440 | tf_op jit(solution)/shard_map/ppermute | solution.py:20
  47.1 5.3 %collective-permute-start.3 = (bf16[1,256,512]{2,1,0:T(8,128)(2,1)S(1)}, bf16[1,256,512]{2,1,0:T(8,128)(2,1)S(1)}, u32[]{:S(2)}, u32[]{:S(2)}) collective-permute-start(bf16[1,256,512]{2,1,0:T(8,128)(2,1)S(1)} %get-tuple-element.40), channel_id=1, source_target_pairs={{1,0},{2,1},{3,2},{4,3},{5,4},{6,5},{7,6},{8,7},{9,8},{10,9},{11,1... | collective-permute-start | bytes 786440 | tf_op jit(solution)/shard_map/ppermute | solution.py:22
  63.0 36.0 %copy-start.2 = (f32[512]{0:T(512)S(1)}, f32[512]{0:T(512)}, u32[]{:S(2)}) copy-start(f32[512]{0:T(512)} %param.14) | copy-start | bytes 6148
  63.0 36.0 %copy-start.3 = (f32[512]{0:T(512)S(1)}, f32[512]{0:T(512)}, u32[]{:S(2)}) copy-start(f32[512]{0:T(512)} %param.13) | copy-start | bytes 6148
  102.0 6.8 %collective-permute-start.4 = (bf16[1,256,512]{2,1,0:T(8,128)(2,1)S(1)}, bf16[1,256,512]{2,1,0:T(8,128)(2,1)S(1)}, u32[]{:S(2)}, u32[]{:S(2)}) collective-permute-start(bf16[1,256,512]{2,1,0:T(8,128)(2,1)S(1)} %get-tuple-element.34), channel_id=1, source_target_pairs={{0,1},{1,2},{2,3},{3,4},{4,5},{5,6},{6,7},{7,8},{8,9},{9,10},{10,1... | collective-permute-start | bytes 786440 | tf_op jit(solution)/shard_map/ppermute | solution.py:20
  103.4 5.3 %collective-permute-start.5 = (bf16[1,256,512]{2,1,0:T(8,128)(2,1)S(1)}, bf16[1,256,512]{2,1,0:T(8,128)(2,1)S(1)}, u32[]{:S(2)}, u32[]{:S(2)}) collective-permute-start(bf16[1,256,512]{2,1,0:T(8,128)(2,1)S(1)} %get-tuple-element.35), channel_id=1, source_target_pairs={{1,0},{2,1},{3,2},{4,3},{5,4},{6,5},{7,6},{8,7},{9,8},{10,9},{11,1... | collective-permute-start | bytes 786440 | tf_op jit(solution)/shard_map/ppermute | solution.py:22
where the time goes:
time: 126 us; the launch traced here: 124 us
  blocking collectives  63.4 us (50%)
  matrix products  22.5 us (18%)
  local copies, waits for them, and re-layouts  14.3 us (11%)
  other arithmetic  11.3 us (9%)
  starting transfers between devices  9.05 us (7%)
  waiting for transfers between devices  3.03 us (2%)
    psum x2, blocking collectives, moments(): lax.psum((jnp.sum(values, axis=(0, 1, 3)), jnp.sum(values * values, axis=...  63.4 us
    dot_general x9, matrix products, convolve(): jnp.dot(stacked.reshape(height * width, 3 * inputs), kernel[row_shift].re...  22.5 us
    slice x3, local copies, waits for them, and re-layouts, convolve(): kernel[row_shift].reshape(3 * inputs, -1)  8.8 us
    ppermute x3, starting transfers between devices, extended(): lax.ppermute(tail, axis, [(i, (i + 1) % count) for i in range(ends)])  5.18 us
    ppermute x3, starting transfers between devices, extended(): lax.ppermute(head, axis, [((i + 1) % count, i) for i in range(ends)])  3.88 us
    convert_element_type x2, other arithmetic, activate(): return jax.nn.silu(normed).astype(jnp.bfloat16)  3.85 us
    slice x3, local copies, waits for them, and re-layouts, convolve(): band[:, col_shift:col_shift + width]  3.7 us
    concatenate x2, other arithmetic, convolve(): jnp.concatenate([band[:, col_shift:col_shift + width] for col_shift in ra...  3.38 us
  transfers between devices with their start and end apart: 6, of which 1 were waited for; matrix products, arithmetic and copies ran while one was open for 7% of the time, Pallas kernels for 0%

commit v1 on v0

v1 whole, which is shorter than its diff:
```python
import functools

import jax
import jax.numpy as jnp
from jax import lax
from jax.experimental import pallas as pl
from jax.experimental.pallas import tpu as pltpu
from jax.sharding import PartitionSpec as P

GROUPS = 32
EPSILON = 1e-06
MESH = pl.DeviceIdType.MESH


def lane_group_sum(values, width):
    lanes = values.shape[1]
    index = lax.broadcasted_iota(jnp.int32, values.shape, 1)
    step = 1
    while step < width:
        up = pltpu.roll(values, step, 1)
        down = pltpu.roll(values, lanes - step, 1)
        values = values + jnp.where((index // step) % 2 == 1, up, down)
        step *= 2
    return values


def shifted(values, amount):
    count = values.shape[0]
    index = lax.broadcasted_iota(jnp.int32, values.shape, 0)
    if amount == 1:
        return jnp.where(index == 0, 0.0, pltpu.roll(values, 1, 0))
    return jnp.where(index == count - 1, 0.0, pltpu.roll(values, count - 1, 0))


def kernel(
    n,
    block,
    latent_ref,
    kin_ref,
    gain_one_ref,
    bias_one_ref,
    gain_two_ref,
    bias_two_ref,
    k1_hbm,
    k2_hbm,
    out_hbm,
    k1,
    k2,
    lat,
    feat,
    stack,
    hid,
    result,
    stat_one,
    stat_two,
    acc,
    weight_sem,
    out_sem,
    lat_send,
    lat_recv,
    hid_send,
    hid_recv,
    one_send,
    one_recv,
    two_send,
    two_recv,
):
    me = lax.axis_index("rows")
    height, channels_in, width = latent_ref.shape
    features = feat.shape[2]
    blocks = height // block
    has_up = me > 0
    has_down = me < n - 1
    up = lax.rem(me + n - 1, n)
    down = lax.rem(me + 1, n)

    barrier = pltpu.get_barrier_semaphore()

    def greet(d, carry):
        pl.semaphore_signal(
            barrier, inc=1, device_id={"rows": lax.rem(me + d, n)}, device_id_type=MESH
        )
        return carry

    lax.fori_loop(1, n, greet, 0)
    fetch_one = pltpu.make_async_copy(k1_hbm, k1, weight_sem.at[0])
    fetch_two = pltpu.make_async_copy(k2_hbm, k2, weight_sem.at[1])
    fetch_one.start()

    def remote(src, dst, send, recv, target):
        return pltpu.make_async_remote_copy(
            src_ref=src,
            dst_ref=dst,
            send_sem=send,
            recv_sem=recv,
            device_id={"rows": target},
            device_id_type=MESH,
        )

    lat[pl.ds(2, height)] = latent_ref[...]

    @pl.when(jnp.logical_not(has_up))
    def _():
        lat[pl.ds(0, 2)] = jnp.zeros((2, channels_in, width), lat.dtype)
        hid[pl.ds(0, 1)] = jnp.zeros((1, width, features), hid.dtype)

    @pl.when(jnp.logical_not(has_down))
    def _():
        lat[pl.ds(height + 2, 2)] = jnp.zeros((2, channels_in, width), lat.dtype)
        hid[pl.ds(height + 1, 1)] = jnp.zeros((1, width, features), hid.dtype)

    column = lax.broadcasted_iota(jnp.int32, (channels_in, width), 1)

    def feature_row(index, count):
        pieces = []
        for a in range(3):
            row = lat[index + a].astype(jnp.float32)
            left = jnp.where(column == 0, 0.0, pltpu.roll(row, 1, 1))
            right = jnp.where(column == width - 1, 0.0, pltpu.roll(row, width - 1, 1))
            for piece in (left, row, right):
                pieces.append(piece.astype(jnp.bfloat16))
        taps = jnp.concatenate(pieces, axis=0)
        row = lax.dot_general(
            taps,
            kin_ref[...],
            (((0,), (0,)), ((), ())),
            preferred_element_type=jnp.float32,
        ).astype(jnp.bfloat16)
        feat[index] = row
        if count:
            add_moments(row)

    def add_moments(row):
        values = row.astype(jnp.float32).reshape(-1, 8, features)
        acc[0] += jnp.sum(values, axis=0)
        acc[1] += jnp.sum(values * values, axis=0)

    def clear_moments():
        acc[...] = jnp.zeros_like(acc)

    def publish(stat, send, recv):
        stat[0] = jnp.sum(acc[...], axis=1)

        def body(d, carry):
            remote(
                stat.at[0], stat.at[d], send.at[d], recv.at[d], lax.rem(me + d, n)
            ).start()
            return carry

        lax.fori_loop(1, n, body, 0)

    def collect(stat, send, recv, gain_ref, bias_ref):
        def body(d, carry):
            remote(
                stat.at[0], stat.at[d], send.at[d], recv.at[d], lax.rem(me + d, n)
            ).wait()
            return carry

        lax.fori_loop(1, n, body, 0)
        totals = jnp.sum(stat[...], axis=0)
        per_group = features // GROUPS
        totals = lane_group_sum(totals, per_group)
        moments = totals / (n * height * width * per_group)
        center = moments[0:1]
        spread = jnp.maximum(moments[1:2] - center * center, 0.0)
        scale = lax.rsqrt(spread + EPSILON) * gain_ref[...]
        return scale, bias_ref[...] - center * scale

    def activate_row(source, index, scale, offset, edge):
        values = source[index].astype(jnp.float32)
        half = (values * scale + offset) * 0.5
        values = half + half * jnp.tanh(half)
        if edge is not None:
            values = jnp.where(edge, values, 0.0)
        stack[index, :, pl.ds(features, features)] = values.astype(jnp.bfloat16)
        stack[index, :, pl.ds(0, features)] = shifted(values, 1).astype(jnp.bfloat16)
        stack[index, :, pl.ds(2 * features, features)] = shifted(values, -1).astype(
            jnp.bfloat16
        )

    def convolve_rows(start, weights):
        total = None
        for a in range(3):
            lhs = stack[pl.ds(start + a, block)].reshape(block * width, 3 * features)
            part = jnp.dot(lhs, weights[a], preferred_element_type=jnp.float32)
            total = part if total is None else total + part
        return total

    lat_up = remote(
        latent_ref.at[pl.ds(0, 2)],
        lat.at[pl.ds(height + 2, 2)],
        lat_send.at[0],
        lat_recv.at[0],
        up,
    )
    lat_down = remote(
        latent_ref.at[pl.ds(height - 2, 2)],
        lat.at[pl.ds(0, 2)],
        lat_send.at[1],
        lat_recv.at[1],
        down,
    )
    pl.semaphore_wait(barrier, n - 1)

    @pl.when(has_up)
    def _():
        lat_up.start()

    @pl.when(has_down)
    def _():
        lat_down.start()

    clear_moments()

    def inner(index, carry):
        feature_row(index, True)
        return carry

    lax.fori_loop(2, height, inner, 0)

    @pl.when(has_up)
    def _():
        lat_up.wait_send()
        lat_down.wait_recv()

    @pl.when(has_down)
    def _():
        lat_down.wait_send()
        lat_up.wait_recv()

    def edge_row(k, carry):
        feature_row(1 + k * (height - 1), True)
        return carry

    lax.fori_loop(0, 2, edge_row, 0)
    publish(stat_one, one_send, one_recv)
    fetch_two.start()

    def halo_row(k, carry):
        feature_row(k * (height + 1), False)
        return carry

    lax.fori_loop(0, 2, halo_row, 0)
    clear_moments()
    scale, offset = collect(stat_one, one_send, one_recv, gain_one_ref, bias_one_ref)

    def first_row(index, carry):
        inside = jnp.logical_and(
            jnp.logical_or(has_up, index > 0), jnp.logical_or(has_down, index < height + 1)
        )
        activate_row(feat, index, scale, offset, inside)
        return carry

    lax.fori_loop(0, height + 2, first_row, 0)
    fetch_one.wait()

    hid_up = remote(hid.at[1], hid.at[height + 1], hid_send.at[0], hid_recv.at[0], up)
    hid_down = remote(hid.at[height], hid.at[0], hid_send.at[1], hid_recv.at[1], down)

    def hidden_block(step, carry):
        start = lax.rem(step + blocks - 1, blocks) * block
        rows = convolve_rows(start, k1).astype(jnp.bfloat16)
        hid[pl.ds(start + 1, block)] = rows.reshape(block, width, features)
        add_moments(rows)

        @pl.when(jnp.logical_and(start == 0, has_up))
        def _():
            hid_up.start()

        @pl.when(jnp.logical_and(start == height - block, has_down))
        def _():
            hid_down.start()

        return carry

    lax.fori_loop(0, blocks, hidden_block, 0)
    publish(stat_two, two_send, two_recv)
    scale, offset = collect(stat_two, two_send, two_recv, gain_two_ref, bias_two_ref)

    def second_row(index, carry):
        activate_row(hid, index, scale, offset, None)
        return carry

    lax.fori_loop(1, height + 1, second_row, 0)

    @pl.when(has_up)
    def _():
        hid_up.wait_send()
        hid_down.wait_recv()

    @pl.when(has_down)
    def _():
        hid_down.wait_send()
        hid_up.wait_recv()

    def second_edge(k, carry):
        inside = jnp.logical_or(
            jnp.logical_and(has_up, k == 0), jnp.logical_and(has_down, k == 1)
        )
        activate_row(hid, k * (height + 1), scale, offset, inside)
        return carry

    lax.fori_loop(0, 2, second_edge, 0)
    fetch_two.wait()

    def store(step):
        return pltpu.make_async_copy(
            result.at[pl.ds(step * block, block)],
            out_hbm.at[pl.ds(step * block, block)],
            out_sem.at[step],
        )

    def final_block(step, carry):
        start = step * block
        rows = convolve_rows(start, k2).reshape(block, width, features)
        rows = rows + feat[pl.ds(start + 1, block)].astype(jnp.float32)
        result[pl.ds(start, block)] = rows.astype(jnp.bfloat16)
        store(step).start()
        return carry

    lax.fori_loop(0, blocks, final_block, 0)

    def drain(step, carry):
        store(step).wait()
        return carry

    lax.fori_loop(0, blocks, drain, 0)


def local(n, latent, kernel_in, gain_one, bias_one, kernel_one, gain_two, bias_two, kernel_two):
    channels_in, height, width = latent.shape
    features = kernel_in.shape[3]
    block = 2 if height % 2 == 0 else 1
    bf16 = jnp.bfloat16
    vmem = pl.BlockSpec(memory_space=pltpu.VMEM)
    hbm = pl.BlockSpec(memory_space=pl.ANY)
    dma = pltpu.SemaphoreType.DMA
    return pl.pallas_call(
        functools.partial(kernel, n, block),
        out_shape=jax.ShapeDtypeStruct((height, width, features), bf16),
        in_specs=[vmem] * 6 + [hbm] * 2,
        out_specs=hbm,
        scratch_shapes=[
            pltpu.VMEM((3, 3 * features, features), bf16),
            pltpu.VMEM((3, 3 * features, features), bf16),
            pltpu.VMEM((height + 4, channels_in, width), bf16),
            pltpu.VMEM((height + 2, width, features), bf16),
            pltpu.VMEM((height + 2, width, 3 * features), bf16),
            pltpu.VMEM((height + 2, width, features), bf16),
            pltpu.VMEM((height, width, features), bf16),
            pltpu.VMEM((n, 2, features), jnp.float32),
            pltpu.VMEM((n, 2, features), jnp.float32),
            pltpu.VMEM((2, 8, features), jnp.float32),
            dma((2,)),
            dma((height // block,)),
            dma((2,)),
            dma((2,)),
            dma((2,)),
            dma((2,)),
            dma((n,)),
            dma((n,)),
            dma((n,)),
            dma((n,)),
        ],
        compiler_params=pltpu.CompilerParams(
            collective_id=0, has_side_effects=True, vmem_limit_bytes=56 * 1024 * 1024
        ),
        name="resblock",
    )(
        jnp.transpose(latent, (1, 0, 2)),
        kernel_in.reshape(9 * channels_in, features),
        gain_one.reshape(1, -1),
        bias_one.reshape(1, -1),
        gain_two.reshape(1, -1),
        bias_two.reshape(1, -1),
        kernel_one.reshape(3, 3 * features, features),
        kernel_two.reshape(3, 3 * features, features),
    )


def solution(mesh):
    in_specs = (P(None, ("batch", "rows"), None), P(), P(), P(), P(), P(), P(), P())
    out_specs = P(("batch", "rows"), None, None)
    return jax.shard_map(
        functools.partial(local, mesh.shape["rows"]),
        mesh=mesh,
        in_specs=in_specs,
        out_specs=out_specs,
        check_vma=False,
    )
```

time: 126 us -> 44.2 us (0.35); the launches traced: 124 us -> 44 us
  blocking collectives: 63.4 us -> 0 us
  Pallas kernels: 0 us -> 41.3 us
  matrix products: 22.5 us -> 0 us
  local copies, waits for them, and re-layouts: 14.3 us -> 2.74 us
  other arithmetic: 11.3 us -> 0 us
  starting transfers between devices: 9.05 us -> 0 us
  waiting for transfers between devices: 3.03 us -> 0 us
    psum x2 -> x0, blocking collectives: 63.4 us -> none  [moments(): lax.psum((jnp.sum(values, axis=(0, 1, 3)), jnp.sum(values * values, axis=...]
    pallas_call x0 -> x1, Pallas kernels: none -> 41.3 us  [local(): pl.pallas_call(functools.partial(kernel, n, block), out_shape=jax.ShapeDt...]
    dot_general x9 -> x0, matrix products: 22.5 us -> none  [convolve(): jnp.dot(stacked.reshape(height * width, 3 * inputs), kernel[row_shift].re...]
    slice x9 -> x0, local copies, waits for them, and re-layouts: 13.3 us -> none  [the longest x3 8.8 us: convolve(): kernel[row_shift].reshape(3 * inputs, -1)]
    ppermute x6 -> x0, starting transfers between devices: 9.05 us -> none  [the longest x3 5.18 us: extended(): lax.ppermute(tail, axis, [(i, (i + 1) % count) for i in range(ends)])]
    convert_element_type x3 -> x0, other arithmetic: 5.54 us -> none  [the longest x2 3.85 us: activate(): return jax.nn.silu(normed).astype(jnp.bfloat16)]
    concatenate x4 -> x0, other arithmetic: 4.43 us -> none  [the longest x2 3.38 us: convolve(): jnp.concatenate([band[:, col_shift:col_shift + width] for col_shift in ra...]
    ppermute x6 -> x0, waiting for transfers between devices: 3.03 us -> none  [the longest x3 3.02 us: extended(): lax.ppermute(head, axis, [((i + 1) % count, i) for i in range(ends)])]
  transfers between devices with their start and end apart: 6 -> 0, of which waited for: 1 -> 0; matrix products, arithmetic and copies ran while one was open for 7% -> 0% of each run, Pallas kernels for 0% -> 0%
where the time goes in v1:
time: 44.2 us; the launch traced here: 44 us
  Pallas kernels  41.3 us (93%)
  local copies, waits for them, and re-layouts  2.74 us (6%)
    pallas_call x1, Pallas kernels, local(): pl.pallas_call(functools.partial(kernel, n, block), out_shape=jax.ShapeDt...  41.3 us
    unnamed x1, local copies, waits for them, and re-layouts  2.74 us

profile of v1, /device:TPU:0, one launch (start us, length us, event | category | flops | bytes accessed | tf_op | source)
XLA Modules:
  0.0 44.0 jit_solution(10620764014641874647)
XLA Ops:
  0.0 41.3 %resblock.1 = bf16[6,256,512]{2,1,0:T(8,128)(2,1)} custom-call(bf16[6,16,256]{2,1,0:T(8,128)(2,1)} %bitcast.11, bf16[144,512]{1,0:T(8,128)(2,1)} %bitcast.10, f32[1,512]{1,0:T(1,128)} %bitcast.12, f32[1,512]{1,0:T(1,128)} %bitcast.13, f32[1,512]{1,0:T(1,128)} %bitcast.14, f32[1,512]{1,0:T(1,128)} %bitcast.15, bf16[3,1536,512]{2,1,0:T(8,128)(2,1)} %bitcast.8, ...), custom_call_target="tpu_custom_call" | custom-call | tf_op jit(solution)/shard_map/resblock/pallas_call | solution.py:338
  41.3 2.7 %copy.10 = bf16[6,256,512]{2,1,0:T(8,128)(2,1)} copy(bf16[6,256,512]{2,1,0:T(8,128)(2,1)} %resblock.1) | data formatting | bytes 3145728

commit v2 on v1

--- a/solution.py
+++ b/solution.py
@@ -24,6 +24,37 @@
     return values
 
 
+def packed(sums):
+    features = sums.shape[1]
+    per_group = features // GROUPS
+    chunks = features // 128
+    sums = lane_group_sum(sums, per_group)
+    slot = lax.broadcasted_iota(jnp.int32, (1, 128), 1) % per_group
+    row = jnp.zeros((1, 128), jnp.float32)
+    for q in range(2):
+        for j in range(chunks):
+            row = jnp.where(
+                slot == q * chunks + j, sums[q : q + 1, 128 * j : 128 * j + 128], row
+            )
+    return row
+
+
+def unpacked(row, features):
+    per_group = features // GROUPS
+    chunks = features // 128
+    shape = (2 * chunks, 128)
+    slot = lax.broadcasted_iota(jnp.int32, shape, 1) % per_group
+    wanted = lax.broadcasted_iota(jnp.int32, shape, 0)
+    rows = jnp.where(slot == wanted, jnp.broadcast_to(row, shape), 0.0)
+    rows = lane_group_sum(rows, per_group)
+    return [
+        jnp.concatenate(
+            [rows[q * chunks + j : q * chunks + j + 1] for j in range(chunks)], axis=1
+        )
+        for q in range(2)
+    ]
+
+
 def shifted(values, amount):
     count = values.shape[0]
     index = lax.broadcasted_iota(jnp.int32, values.shape, 0)
@@ -35,27 +66,31 @@
 def kernel(
     n,
     block,
-    latent_ref,
+    latent_hbm,
+    kin_hbm,
+    gain_one_hbm,
+    bias_one_hbm,
+    gain_two_hbm,
+    bias_two_hbm,
+    k1_hbm,
+    k2_hbm,
+    result,
     kin_ref,
     gain_one_ref,
     bias_one_ref,
     gain_two_ref,
     bias_two_ref,
-    k1_hbm,
-    k2_hbm,
-    out_hbm,
     k1,
     k2,
     lat,
     feat,
     stack,
     hid,
-    result,
     stat_one,
     stat_two,
     acc,
     weight_sem,
-    out_sem,
+    small_sem,
     lat_send,
     lat_recv,
     hid_send,
@@ -66,7 +101,7 @@
     two_recv,
 ):
     me = lax.axis_index("rows")
-    height, channels_in, width = latent_ref.shape
+    height, channels_in, width = latent_hbm.shape
     features = feat.shape[2]
     blocks = height // block
     has_up = me > 0
@@ -85,6 +120,21 @@
     lax.fori_loop(1, n, greet, 0)
     fetch_one = pltpu.make_async_copy(k1_hbm, k1, weight_sem.at[0])
     fetch_two = pltpu.make_async_copy(k2_hbm, k2, weight_sem.at[1])
+    small = [
+        pltpu.make_async_copy(src, dst, small_sem.at[i])
+        for i, (src, dst) in enumerate(
+            (
+                (latent_hbm, lat.at[pl.ds(2, height)]),
+                (kin_hbm, kin_ref),
+                (gain_one_hbm, gain_one_ref),
+                (bias_one_hbm, bias_one_ref),
+                (gain_two_hbm, gain_two_ref),
+                (bias_two_hbm, bias_two_ref),
+            )
+        )
+    ]
+    for copy in small:
+        copy.start()
     fetch_one.start()
 
     def remote(src, dst, send, recv, target):
@@ -96,8 +146,6 @@
             device_id={"rows": target},
             device_id_type=MESH,
         )
-
-    lat[pl.ds(2, height)] = latent_ref[...]
 
     @pl.when(jnp.logical_not(has_up))
     def _():
@@ -139,7 +187,7 @@
         acc[...] = jnp.zeros_like(acc)
 
     def publish(stat, send, recv):
-        stat[0] = jnp.sum(acc[...], axis=1)
+        stat[0] = packed(jnp.sum(acc[...], axis=1))
 
         def body(d, carry):
             remote(
@@ -157,12 +205,10 @@
             return carry
 
         lax.fori_loop(1, n, body, 0)
-        totals = jnp.sum(stat[...], axis=0)
-        per_group = features // GROUPS
-        totals = lane_group_sum(totals, per_group)
-        moments = totals / (n * height * width * per_group)
-        center = moments[0:1]
-        spread = jnp.maximum(moments[1:2] - center * center, 0.0)
+        row = jnp.sum(stat[...].reshape(n, 128), axis=0, keepdims=True)
+        count = n * height * width * (features // GROUPS)
+        center, square = [total / count for total in unpacked(row, features)]
+        spread = jnp.maximum(square - center * center, 0.0)
         scale = lax.rsqrt(spread + EPSILON) * gain_ref[...]
         return scale, bias_ref[...] - center * scale
 
@@ -187,19 +233,21 @@
         return total
 
     lat_up = remote(
-        latent_ref.at[pl.ds(0, 2)],
+        lat.at[pl.ds(2, 2)],
         lat.at[pl.ds(height + 2, 2)],
         lat_send.at[0],
         lat_recv.at[0],
         up,
     )
     lat_down = remote(
-        latent_ref.at[pl.ds(height - 2, 2)],
+        lat.at[pl.ds(height, 2)],
         lat.at[pl.ds(0, 2)],
         lat_send.at[1],
         lat_recv.at[1],
         down,
     )
+    for copy in small:
+        copy.wait()
     pl.semaphore_wait(barrier, n - 1)
 
     @pl.when(has_up)
@@ -244,87 +292,102 @@
     clear_moments()
     scale, offset = collect(stat_one, one_send, one_recv, gain_one_ref, bias_one_ref)
 
-    def first_row(index, carry):
-        inside = jnp.logical_and(
-            jnp.logical_or(has_up, index > 0), jnp.logical_or(has_down, index < height + 1)
-        )
-        activate_row(feat, index, scale, offset, inside)
-        return carry
-
-    lax.fori_loop(0, height + 2, first_row, 0)
-    fetch_one.wait()
+    def inside(index):
+        if index == 0:
+            return has_up
+        if index == height + 1:
+            return has_down
+        return None
+
+    def rows_of(number):
+        return range(number * block, number * block + block + 2)
+
+    def run_blocks(source, order, scale, offset, before_halo, ready, emit):
+        done = set()
+        halo_ready = False
+
+        def fill(indices):
+            nonlocal halo_ready
+            for index in indices:
+                if index in done:
+                    continue
+                if inside(index) is not None and not halo_ready:
+                    before_halo()
+                    halo_ready = True
+                done.add(index)
+                activate_row(source, index, scale, offset, inside(index))
+
+        fill(rows_of(order[0]))
+        ready()
+        for step, number in enumerate(order):
+            following = rows_of(order[step + 1]) if step + 1 < len(order) else ()
+            new = [index for index in following if index not in done]
+            if not halo_ready and any(inside(index) is not None for index in new):
+                before_halo()
+                halo_ready = True
+            emit(number, lambda: fill(new))
 
     hid_up = remote(hid.at[1], hid.at[height + 1], hid_send.at[0], hid_recv.at[0], up)
     hid_down = remote(hid.at[height], hid.at[0], hid_send.at[1], hid_recv.at[1], down)
 
-    def hidden_block(step, carry):
-        start = lax.rem(step + blocks - 1, blocks) * block
+    def hidden_block(number, beside):
+        start = number * block
         rows = convolve_rows(start, k1).astype(jnp.bfloat16)
+        beside()
         hid[pl.ds(start + 1, block)] = rows.reshape(block, width, features)
         add_moments(rows)
-
-        @pl.when(jnp.logical_and(start == 0, has_up))
-        def _():
-            hid_up.start()
-
-        @pl.when(jnp.logical_and(start == height - block, has_down))
-        def _():
-            hid_down.start()
-
-        return carry
-
-    lax.fori_loop(0, blocks, hidden_block, 0)
+        if start == 0:
+
+            @pl.when(has_up)
+            def _():
+                hid_up.start()
+
+        if start == height - block:
+
+            @pl.when(has_down)
+            def _():
+                hid_down.start()
+
+    last = blocks - 1
+    run_blocks(
+        feat,
+        [last] + list(range(last)),
+        scale,
+        offset,
+        lambda: None,
+        fetch_one.wait,
+        hidden_block,
+    )
     publish(stat_two, two_send, two_recv)
     scale, offset = collect(stat_two, two_send, two_recv, gain_two_ref, bias_two_ref)
 
-    def second_row(index, carry):
-        activate_row(hid, index, scale, offset, None)
-        return carry
-
-    lax.fori_loop(1, height + 1, second_row, 0)
-
-    @pl.when(has_up)
-    def _():
-        hid_up.wait_send()
-        hid_down.wait_recv()
-
-    @pl.when(has_down)
-    def _():
-        hid_down.wait_send()
-        hid_up.wait_recv()
-
-    def second_edge(k, carry):
-        inside = jnp.logical_or(
-            jnp.logical_and(has_up, k == 0), jnp.logical_and(has_down, k == 1)
-        )
-        activate_row(hid, k * (height + 1), scale, offset, inside)
-        return carry
-
-    lax.fori_loop(0, 2, second_edge, 0)
-    fetch_two.wait()
-
-    def store(step):
-        return pltpu.make_async_copy(
-            result.at[pl.ds(step * block, block)],
-            out_hbm.at[pl.ds(step * block, block)],
-            out_sem.at[step],
-        )
-
-    def final_block(step, carry):
-        start = step * block
+    def wait_hidden():
+        @pl.when(has_up)
+        def _():
+            hid_up.wait_send()
+            hid_down.wait_recv()
+
+        @pl.when(has_down)
+        def _():
+            hid_down.wait_send()
+            hid_up.wait_recv()
+
+    def final_block(number, beside):
+        start = number * block
         rows = convolve_rows(start, k2).reshape(block, width, features)
+        beside()
         rows = rows + feat[pl.ds(start + 1, block)].astype(jnp.float32)
         result[pl.ds(start, block)] = rows.astype(jnp.bfloat16)
-        store(step).start()
-        return carry
-
-    lax.fori_loop(0, blocks, final_block, 0)
-
-    def drain(step, carry):
-        store(step).wait()
-        return carry
-
-    lax.fori_loop(0, blocks, drain, 0)
+
+    run_blocks(
+        hid,
+        list(range(1, blocks)) + [0],
+        scale,
+        offset,
+        wait_hidden,
+        fetch_two.wait,
+        final_block,
+    )
 
 
 def local(n, latent, kernel_in, gain_one, bias_one, kernel_one, gain_two, bias_two, kernel_two):
@@ -337,22 +400,26 @@
     dma = pltpu.SemaphoreType.DMA
     return pl.pallas_call(
         functools.partial(kernel, n, block),
-        out_shape=jax.ShapeDtypeStruct((height, width, features), bf16),
-        in_specs=[vmem] * 6 + [hbm] * 2,
-        out_specs=hbm,
+        out_shape=pltpu.VMEM((height, width, features), bf16),
+        in_specs=[hbm] * 8,
+        out_specs=vmem,
         scratch_shapes=[
+            pltpu.VMEM((9 * channels_in, features), bf16),
+            pltpu.VMEM((1, features), jnp.float32),
+            pltpu.VMEM((1, features), jnp.float32),
+            pltpu.VMEM((1, features), jnp.float32),
+            pltpu.VMEM((1, features), jnp.float32),
             pltpu.VMEM((3, 3 * features, features), bf16),
             pltpu.VMEM((3, 3 * features, features), bf16),
             pltpu.VMEM((height + 4, channels_in, width), bf16),
             pltpu.VMEM((height + 2, width, features), bf16),
             pltpu.VMEM((height + 2, width, 3 * features), bf16),
             pltpu.VMEM((height + 2, width, features), bf16),
-            pltpu.VMEM((height, width, features), bf16),
-            pltpu.VMEM((n, 2, features), jnp.float32),
-            pltpu.VMEM((n, 2, features), jnp.float32),
+            pltpu.VMEM((n, 1, 128), jnp.float32),
+            pltpu.VMEM((n, 1, 128), jnp.float32),
             pltpu.VMEM((2, 8, features), jnp.float32),
             dma((2,)),
-            dma((height // block,)),
+            dma((6,)),
             dma((2,)),
             dma((2,)),
             dma((2,)),

time: 44.2 us -> 39.7 us (0.90)
  Pallas kernels: 41.3 us -> 38.4 us
  local copies, waits for them, and re-layouts: 2.74 us -> 1.15 us
    pallas_call x1, Pallas kernels: 41.3 us -> 38.4 us  [local(): pl.pallas_call(functools.partial(kernel, n, block), out_shape=pltpu.VMEM(...]
    unnamed x1, local copies, waits for them, and re-layouts: 2.74 us -> 1.15 us
where the time goes in v2:
time: 39.7 us; the launch traced here: 39.6 us
  Pallas kernels  38.4 us (97%)
  local copies, waits for them, and re-layouts  1.15 us (3%)
    pallas_call x1, Pallas kernels, local(): pl.pallas_call(functools.partial(kernel, n, block), out_shape=pltpu.VMEM(...  38.4 us
    unnamed x1, local copies, waits for them, and re-layouts  1.15 us

profile of v2, /device:TPU:0, one launch (start us, length us, event | category | flops | bytes accessed | tf_op | source)
XLA Modules:
  0.0 39.6 jit_solution(13682050104393222608)
XLA Ops:
  0.0 38.4 %resblock.1 = bf16[6,256,512]{2,1,0:T(8,128)(2,1)S(1)} custom-call(bf16[6,16,256]{2,1,0:T(8,128)(2,1)} %bitcast.11, bf16[144,512]{1,0:T(8,128)(2,1)} %bitcast.10, f32[1,512]{1,0:T(1,128)} %bitcast.12, f32[1,512]{1,0:T(1,128)} %bitcast.13, f32[1,512]{1,0:T(1,128)} %bitcast.14, f32[1,512]{1,0:T(1,128)} %bitcast.15, bf16[3,1536,512]{2,1,0:T(8,128)(2,1)} %bitcast.8, ...), custom_call_target="tpu_custom_call" | custom-call | tf_op jit(solution)/shard_map/resblock/pallas_call | solution.py:401
  38.4 1.1 %copy.10 = bf16[6,256,512]{2,1,0:T(8,128)(2,1)} copy(bf16[6,256,512]{2,1,0:T(8,128)(2,1)S(1)} %resblock.1) | data formatting | bytes 3145728

commit v3 on v2

--- a/solution.py
+++ b/solution.py
@@ -302,29 +302,20 @@
     def rows_of(number):
         return range(number * block, number * block + block + 2)
 
-    def run_blocks(source, order, scale, offset, before_halo, ready, emit):
+    def run_blocks(source, order, scale, offset, ready, emit):
         done = set()
-        halo_ready = False
 
         def fill(indices):
-            nonlocal halo_ready
             for index in indices:
-                if index in done:
-                    continue
-                if inside(index) is not None and not halo_ready:
-                    before_halo()
-                    halo_ready = True
-                done.add(index)
-                activate_row(source, index, scale, offset, inside(index))
-
+                if index not in done:
+                    done.add(index)
+                    activate_row(source, index, scale, offset, inside(index))
+
+        ready()
         fill(rows_of(order[0]))
-        ready()
         for step, number in enumerate(order):
             following = rows_of(order[step + 1]) if step + 1 < len(order) else ()
             new = [index for index in following if index not in done]
-            if not halo_ready and any(inside(index) is not None for index in new):
-                before_halo()
-                halo_ready = True
             emit(number, lambda: fill(new))
 
     hid_up = remote(hid.at[1], hid.at[height + 1], hid_send.at[0], hid_recv.at[0], up)
@@ -354,7 +345,6 @@
         [last] + list(range(last)),
         scale,
         offset,
-        lambda: None,
         fetch_one.wait,
         hidden_block,
     )
@@ -362,6 +352,8 @@
     scale, offset = collect(stat_two, two_send, two_recv, gain_two_ref, bias_two_ref)
 
     def wait_hidden():
+        fetch_two.wait()
+
         @pl.when(has_up)
         def _():
             hid_up.wait_send()
@@ -385,7 +377,6 @@
         scale,
         offset,
         wait_hidden,
-        fetch_two.wait,
         final_block,
     )
 

time: 39.7 us -> 37.5 us (0.945)
  Pallas kernels: 38.4 us -> 36.2 us
    pallas_call x1, Pallas kernels: 38.4 us -> 36.2 us  [local(): pl.pallas_call(functools.partial(kernel, n, block), out_shape=pltpu.VMEM(...]
where the time goes in v3:
time: 37.5 us; the launch traced here: 37.3 us
  Pallas kernels  36.2 us (97%)
  local copies, waits for them, and re-layouts  1.15 us (3%)
    pallas_call x1, Pallas kernels, local(): pl.pallas_call(functools.partial(kernel, n, block), out_shape=pltpu.VMEM(...  36.2 us
    unnamed x1, local copies, waits for them, and re-layouts  1.15 us

profile of v3, /device:TPU:0, one launch (start us, length us, event | category | flops | bytes accessed | tf_op | source)
XLA Modules:
  0.0 37.3 jit_solution(16135399453215077610)
XLA Ops:
  0.0 36.2 %resblock.1 = bf16[6,256,512]{2,1,0:T(8,128)(2,1)S(1)} custom-call(bf16[6,16,256]{2,1,0:T(8,128)(2,1)} %bitcast.11, bf16[144,512]{1,0:T(8,128)(2,1)} %bitcast.10, f32[1,512]{1,0:T(1,128)} %bitcast.12, f32[1,512]{1,0:T(1,128)} %bitcast.13, f32[1,512]{1,0:T(1,128)} %bitcast.14, f32[1,512]{1,0:T(1,128)} %bitcast.15, bf16[3,1536,512]{2,1,0:T(8,128)(2,1)} %bitcast.8, ...), custom_call_target="tpu_custom_call" | custom-call | tf_op jit(solution)/shard_map/resblock/pallas_call | solution.py:392
  36.2 1.1 %copy.10 = bf16[6,256,512]{2,1,0:T(8,128)(2,1)} copy(bf16[6,256,512]{2,1,0:T(8,128)(2,1)S(1)} %resblock.1) | data formatting | bytes 3145728
